TPU v7x, 32 devices: a whole 2x2x4 slice. The times are simulated.
32 devices in a mesh: rows: 4 (over y, x), mp: 8 (over z, core).
Axes of the slice: x: 2, y: 2, z: 4, core: 2. Of those that a mesh axis runs over, the one named last changes fastest.
Arguments:
- tokens: bfloat16 [512, 6144], P('rows', 'mp'), may hold values from -8 to 8
- norm_gain: float32 [6144], replicated, may hold values from 0.25 to 1.75
- hidden_bias: float32 [24576], P('mp'), may hold values from -3 to 3
- weight_in: bfloat16 [6144, 24576], P('rows', 'mp'), may hold values from -0.078125 to 0.078125
- weight_out: bfloat16 [24576, 6144], P('mp', 'rows'), may hold values from -0.0546875 to 0.0546875
Outputs:
- updated: bfloat16 [512, 6144], P('rows', 'mp')
All inputs are finite; a program needn't handle non-finite values.
Results may differ from a plain program's by a relative error of at most 0.0041.
Values may be sent and summed in bfloat16 or wider, within the bound.
A program may use at most 128 MiB of HBM per device.

v0:
```python
import jax
import jax.numpy as jnp
from jax import lax
from jax.sharding import PartitionSpec as P

D = 6144
floor_value = 0.1


def normalize(as_float, moment_sum, square_sum, gain, width):
    row_mean = moment_sum / width
    row_var = jnp.maximum(square_sum / width - row_mean * row_mean, 0.0)
    inverse = lax.rsqrt(row_var + floor_value)
    return ((as_float - row_mean[:, None]) * inverse[:, None] * gain[None, :]).astype(jnp.bfloat16)


def body(tokens, norm_gain, hidden_bias, weight_in, weight_out):
    as_float = tokens.astype(jnp.float32)
    moment_sum, square_sum = lax.psum(
        (jnp.sum(as_float, axis=1), jnp.sum(as_float * as_float, axis=1)), "mp"
    )
    local_gain = lax.dynamic_slice_in_dim(
        norm_gain, lax.axis_index("mp") * tokens.shape[1], tokens.shape[1]
    )
    shard_norm = normalize(as_float, moment_sum, square_sum, local_gain, D)
    normed = lax.all_gather(shard_norm, "mp", axis=1, tiled=True)
    shuffled = lax.all_to_all(normed, "rows", split_axis=1, concat_axis=0, tiled=True)
    preact = lax.psum_scatter(
        jnp.dot(shuffled, weight_in, preferred_element_type=jnp.float32),
        "rows",
        scatter_dimension=0,
        tiled=True,
    )
    hidden = jax.nn.gelu(preact + hidden_bias[None, :], approximate=False).astype(jnp.bfloat16)
    terms = jnp.dot(
        hidden,
        lax.all_gather(weight_out, "rows", axis=1, tiled=True),
        preferred_element_type=jnp.float32,
    )
    branch = lax.psum_scatter(terms, "mp", scatter_dimension=1, tiled=True)
    return (as_float + branch).astype(jnp.bfloat16)


def solution(mesh):
    return jax.shard_map(
        body,
        mesh=mesh,
        in_specs=(P("rows", "mp"), P(), P("mp"), P("rows", "mp"), P("mp", "rows")),
        out_specs=P("rows", "mp"),
        check_vma=False,
    )
```

profile of v0, /device:TPU:0, one launch (start us, length us, event | category | flops | bytes accessed | tf_op | source)
XLA Modules:
  0.0 561.1 jit_solution(460465434844182383)
XLA Ops:
  6.5 0.0 all-gather.3.cloned.1.call-start
  6.5 1.1 convert_reduce_fusion
  7.6 18.1 %all-reduce = (f32[128]{0:T(128)S(1)}, f32[128]{0:T(128)S(1)}) all-reduce(f32[128]{0:T(128)S(1)} %get-tuple-element.6, f32[128]{0:T(128)S(1)} %get-tuple-element.5), channel_id=1, replica_groups=mesh['rows'=4,'mp'=8] {'mp'}, use_global_device_ids=true, to_apply=%region_3.0 | all-reduce | flops 256 | bytes 2048 | tf_op jit(solution)/shard_map/psum | solution.py:19
  25.7 0.8 dynamic_slice.3
  26.5 1.8 fusion.45
  28.3 0.0 all-gather.3.cloned.1.call-update
  28.3 0.0 reduce-scatter.3.cloned.1.call-start
  28.3 23.6 %all-gather.3.cloned.1.call-done = bf16[128,6144]{1,0:T(8,128)(2,1)} async-done(((bf16[128,768]{1,0:T(8,128)(2,1)}), bf16[128,6144]{1,0:T(8,128)(2,1)}) %all-gather.3.cloned.1.call-update) | async-done | bytes 1572880 | tf_op jit(solution)/shard_map/all_gather | solution.py:26
  51.9 1.5 copy.9
  53.4 23.6 %all_to_all.19 = bf16[128,4,1536]{2,0,1:T(8,128)(2,1)S(1)} all-to-all(bf16[128,4,1536]{2,0,1:T(8,128)(2,1)S(1)} %bitcast.10), channel_id=1, replica_groups=mesh['rows'=4,'mp'=8] {'rows'}, dimensions={1} | all-to-all | bytes 3145728 | tf_op jit(solution)/shard_map/all_to_all | solution.py:27
  77.0 10.6 %fusion.78 = f32[512,3072]{1,0:T(8,128)} fusion(bf16[512,1536]{1,0:T(8,128)(2,1)S(1)} %bitcast.12, bf16[1536,3072]{1,0:T(8,128)(2,1)} %param.8), kind=kOutput, calls=%fused_computation.93 | convolution fusion | flops 4831838208 | bytes 17301504 | tf_op jit(solution)/shard_map/dot_general | solution.py:29
  87.6 0.0 reduce-scatter.3.cloned.1.call-update
  87.6 0.0 copy-start.1
  87.6 0.0 all-gather.5.cloned.1.call-start
  87.7 0.7 all-gather.5.cloned.1.call-update
  88.4 0.0 reduce-scatter.5.cloned.1.call-start
  88.4 67.0 %reduce-scatter.3.cloned.1.call-done = f32[128,3072]{1,0:T(8,128)} async-done(((f32[512,3072]{1,0:T(8,128)}), f32[128,3072]{1,0:T(8,128)}) %reduce-scatter.3.cloned.1.call-update) | async-done | bytes 1572880 | tf_op jit(solution)/shard_map/reduce_scatter | solution.py:28
  155.5 334.7 %all-gather.5.cloned.1.call-done = bf16[3072,6144]{1,0:T(8,128)(2,1)} async-done(((bf16[3072,1536]{1,0:T(8,128)(2,1)}), bf16[3072,6144]{1,0:T(8,128)(2,1)}) %all-gather.5.cloned.1.call-update) | async-done | bytes 37748752 | tf_op jit(solution)/shard_map/all_gather | solution.py:37
  490.2 0.0 copy-done.1
  490.2 22.1 %fusion.10 = f32[128,6144]{1,0:T(8,128)} fusion(bf16[3072,6144]{1,0:T(8,128)(2,1)} %all-gather.5.cloned.1.call-done, f32[128,3072]{1,0:T(8,128)} %reduce-scatter.3.cloned.1.call-done, f32[3072]{0:T(1024)S(1)} %copy-done.1), kind=kOutput, calls=%fused_computation.20 | convolution fusion | flops 4857790464 | bytes 42479616 | tf_op jit(solution)/shard_map/dot_general | solution.py:35
  512.3 0.0 copy-start
  512.3 0.0 reduce-scatter.5.cloned.1.call-update
  512.3 40.5 %reduce-scatter.5.cloned.1.call-done = f32[128,768]{1,0:T(8,128)} async-done(((f32[128,6144]{1,0:T(8,128)}), f32[128,768]{1,0:T(8,128)}) %reduce-scatter.5.cloned.1.call-update) | async-done | bytes 393232 | tf_op jit(solution)/shard_map/reduce_scatter | solution.py:40
  552.8 0.0 copy-done
  552.8 1.7 fusion.47
  (1 shorter events, 0.0 us)
Async XLA Ops:
  6.5 45.4 %all-gather.3.cloned.1.call-start = ((), (), s32[]{:S(2)}) async-start(), calls=%async_computation.3 | async-start | bytes 1769472 | tf_op jit(solution)/shard_map/all_gather | solution.py:26
  28.3 127.2 %reduce-scatter.3.cloned.1.call-start = ((), (), s32[]{:S(2)}) async-start(), calls=%async_computation.4 | async-start | bytes 7864320 | tf_op jit(solution)/shard_map/reduce_scatter | solution.py:28
  87.6 402.6 %copy-start.1 = (f32[3072]{0:T(1024)S(1)}, f32[3072]{0:T(1024)}, u32[]{:S(2)}) copy-start(f32[3072]{0:T(1024)} %param.7) | copy-start | bytes 36868
  87.6 402.6 %all-gather.5.cloned.1.call-start = ((), (), s32[]{:S(2)}) async-start(), calls=%async_computation.5 | async-start | bytes 47185920 | tf_op jit(solution)/shard_map/all_gather | solution.py:37
  88.4 464.4 %reduce-scatter.5.cloned.1.call-start = ((), (), s32[]{:S(2)}) async-start(), calls=%async_computation.6 | async-start | bytes 3538944 | tf_op jit(solution)/shard_map/reduce_scatter | solution.py:40
  512.3 40.6 %copy-start = (bf16[128,768]{1,0:T(8,128)(2,1)S(1)}, bf16[128,768]{1,0:T(8,128)(2,1)}, u32[]{:S(2)}) copy-start(bf16[128,768]{1,0:T(8,128)(2,1)} %param.5) | copy-start | bytes 589828
Sparse Core Ops, SparseCore 0:
  28.4 23.4 all-gather.2
  87.7 67.6 reduce-scatter.2
  157.3 332.8 all-gather.4
  512.4 40.3 reduce-scatter.4
where the time goes:
time: 561 us
  waiting for transfers between devices  467 us (83%)
  blocking collectives  41.7 us (7%)
  matrix products  32.6 us (6%)
  between operations  13.2 us (2%)
    all_gather x1, waiting for transfers between devices, body(): lax.all_gather(weight_out, 'rows', axis=1, tiled=True)  335 us
    reduce_scatter x1, waiting for transfers between devices, body(): lax.psum_scatter(jnp.dot(shuffled, weight_in, preferred_element_type=jnp....  67 us
    reduce_scatter x1, waiting for transfers between devices, body(): branch = lax.psum_scatter(terms, 'mp', scatter_dimension=1, tiled=True)  40.5 us
    all_to_all x1, blocking collectives, body(): lax.all_to_all(normed, 'rows', split_axis=1, concat_axis=0, tiled=True)  23.6 us
    all_gather x1, waiting for transfers between devices, body(): normed = lax.all_gather(shard_norm, 'mp', axis=1, tiled=True)  23.6 us
    dot_general x1, matrix products, body(): jnp.dot(hidden, lax.all_gather(weight_out, 'rows', axis=1, tiled=True), p...  22.1 us
    psum x1, blocking collectives, body(): lax.psum((jnp.sum(as_float, axis=1), jnp.sum(as_float * as_float, axis=1)...  18.1 us
  transfers between devices with their start and end apart: 4, of which 4 were waited for; matrix products, arithmetic and copies ran while one was open for 0% of the time, Pallas kernels for 0%

commit v1 on v0

--- a/solution.py
+++ b/solution.py
@@ -2,9 +2,22 @@
 import jax.numpy as jnp
 from jax import lax
 from jax.sharding import PartitionSpec as P
+from jax.lax import axis_index, ppermute, psum
 
 D = 6144
 floor_value = 0.1
+
+
+def clear_pages(chunk, mesh_dim):
+    y2, new = (psum(1, mesh_dim), axis_index(mesh_dim))
+    formed, t1 = (chunk, 1)
+    while t1 < y2:
+        carry = ppermute(formed, mesh_dim, [(rr, rr ^ t1) for rr in range(y2)])
+        low = jnp.concatenate([formed, carry], 1)
+        raw_out = jnp.concatenate([carry, formed], axis=1)
+        formed = jnp.where(new & t1 == 0, low, raw_out)
+        t1 = 2 * t1
+    return formed
 
 
 def normalize(as_float, moment_sum, square_sum, gain, width):
@@ -32,11 +45,7 @@
         tiled=True,
     )
     hidden = jax.nn.gelu(preact + hidden_bias[None, :], approximate=False).astype(jnp.bfloat16)
-    terms = jnp.dot(
-        hidden,
-        lax.all_gather(weight_out, "rows", axis=1, tiled=True),
-        preferred_element_type=jnp.float32,
-    )
+    terms = jnp.dot(hidden, clear_pages(weight_out, "rows"), preferred_element_type=jnp.float32)
     branch = lax.psum_scatter(terms, "mp", scatter_dimension=1, tiled=True)
     return (as_float + branch).astype(jnp.bfloat16)
 

time: 561 us -> 825 us (1.47)
  blocking collectives: 41.7 us -> 396 us
  waiting for transfers between devices: 467 us -> 338 us
  other arithmetic: 4.54 us -> 23 us
  matrix products: 32.6 us -> 48.2 us
    all_to_all x1, blocking collectives: 23.6 us -> 380 us  [body(): lax.all_to_all(normed, 'rows', split_axis=1, concat_axis=0, tiled=True)]
    all_gather x1 -> x0, waiting for transfers between devices: 335 us -> none  [body(): lax.all_gather(weight_out, 'rows', axis=1, tiled=True)]
    ppermute x0 -> x2, waiting for transfers between devices: none -> 203 us  [clear_pages(): carry = ppermute(formed, mesh_dim, [(rr, rr ^ t1) for rr in range(y2)])]
    select_n x0 -> x1, other arithmetic: none -> 20.3 us  [clear_pages(): formed = jnp.where(new & t1 == 0, low, raw_out)]
    dot_general x1, matrix products: 22.1 us -> 37.7 us  [body(): jnp.dot(hidden, clear_pages(weight_out, 'rows'), preferred_element_type=j...]
  transfers between devices with their start and end apart: 4 -> 5, of which waited for: 4 -> 4; matrix products, arithmetic and copies ran while one was open for 0% -> 2% of each run, Pallas kernels for 0% -> 0%
where the time goes in v1:
time: 825 us
  blocking collectives  396 us (48%)
  waiting for transfers between devices  338 us (41%)
  matrix products  48.2 us (6%)
  other arithmetic  23 us (3%)
  between operations  13.1 us (2%)
    all_to_all x1, blocking collectives, body(): lax.all_to_all(normed, 'rows', split_axis=1, concat_axis=0, tiled=True)  380 us
    ppermute x2, waiting for transfers between devices, clear_pages(): carry = ppermute(formed, mesh_dim, [(rr, rr ^ t1) for rr in range(y2)])  203 us
    reduce_scatter x1, waiting for transfers between devices, body(): lax.psum_scatter(jnp.dot(shuffled, weight_in, preferred_element_type=jnp....  71.3 us
    reduce_scatter x1, waiting for transfers between devices, body(): branch = lax.psum_scatter(terms, 'mp', scatter_dimension=1, tiled=True)  40.5 us
    dot_general x1, matrix products, body(): jnp.dot(hidden, clear_pages(weight_out, 'rows'), preferred_element_type=j...  37.7 us
    all_gather x1, waiting for transfers between devices, body(): normed = lax.all_gather(shard_norm, 'mp', axis=1, tiled=True)  22.6 us
    select_n x1, other arithmetic, clear_pages(): formed = jnp.where(new & t1 == 0, low, raw_out)  20.3 us
  transfers between devices with their start and end apart: 5, of which 4 were waited for; matrix products, arithmetic and copies ran while one was open for 2% of the time, Pallas kernels for 0%

profile of v1, /device:TPU:0, one launch (start us, length us, event | category | flops | bytes accessed | tf_op | source)
XLA Modules:
  0.0 824.9 jit_solution(16975063714818692615)
XLA Ops:
  6.5 0.0 all-gather.2.cloned.1.call-start
  6.5 3.0 collective-permute-start
  9.5 0.0 copy-start
  9.5 203.2 %collective-permute-done = bf16[3072,1536]{1,0:T(8,128)(2,1)} collective-permute-done((bf16[3072,1536]{1,0:T(8,128)(2,1)}, bf16[3072,1536]{1,0:T(8,128)(2,1)}, u32[]{:S(2)}, u32[]{:S(2)}) %collective-permute-start) | collective-permute-done | bytes 9437216 | tf_op jit(solution)/shard_map/ppermute | solution.py:15
  212.7 20.3 %maximum_select_fusion.2 = bf16[3072,3072]{1,0:T(8,128)(2,1)} fusion(bf16[3072,1536]{1,0:T(8,128)(2,1)} %collective-permute-done, bf16[3072,1536]{1,0:T(8,128)(2,1)} %param.9, pred[]{:T(512)S(6)} %eq.7), kind=kLoop, calls=%fused_computation.8 | loop fusion | flops 84934656 | bytes 37748736 | tf_op jit(solution)/shard_map/jit(_where)/select_n | solution.py:18
  233.1 1.8 collective-permute-start.1
  234.9 0.8 dynamic_slice.3
  235.7 0.0 copy-done
  235.7 0.1 convert_reduce_fusion
  235.8 15.5 %all-reduce = (f32[128]{0:T(128)S(1)}, f32[128]{0:T(128)S(1)}) all-reduce(f32[128]{0:T(128)S(1)} %get-tuple-element.6, f32[128]{0:T(128)S(1)} %get-tuple-element.5), channel_id=1, replica_groups=mesh['rows'=4,'mp'=8] {'mp'}, use_global_device_ids=true, to_apply=%region_3.0 | all-reduce | flops 256 | bytes 2048 | tf_op jit(solution)/shard_map/psum | solution.py:32
  251.3 0.8 fusion.51
  252.1 0.0 all-gather.2.cloned.1.call-update
  252.2 0.0 reduce-scatter.3.cloned.1.call-start
  252.2 22.6 %all-gather.2.cloned.1.call-done = bf16[128,6144]{1,0:T(8,128)(2,1)} async-done(((bf16[128,768]{1,0:T(8,128)(2,1)}), bf16[128,6144]{1,0:T(8,128)(2,1)}) %all-gather.2.cloned.1.call-update) | async-done | bytes 1572880 | tf_op jit(solution)/shard_map/all_gather | solution.py:39
  274.8 1.5 copy.9
  276.4 380.1 %all_to_all.19 = bf16[128,4,1536]{2,0,1:T(8,128)(2,1)S(1)} all-to-all(bf16[128,4,1536]{2,0,1:T(8,128)(2,1)S(1)} %bitcast.9), channel_id=1, replica_groups=mesh['rows'=4,'mp'=8] {'rows'}, dimensions={1} | all-to-all | bytes 3145728 | tf_op jit(solution)/shard_map/all_to_all | solution.py:40
  656.5 10.6 %fusion.85 = f32[512,3072]{1,0:T(8,128)} fusion(bf16[512,1536]{1,0:T(8,128)(2,1)S(1)} %bitcast.11, bf16[1536,3072]{1,0:T(8,128)(2,1)} %param.8), kind=kOutput, calls=%fused_computation.102 | convolution fusion | flops 4831838208 | bytes 17301504 | tf_op jit(solution)/shard_map/dot_general | solution.py:42
  667.1 0.0 copy-start.1
  667.1 0.0 reduce-scatter.3.cloned.1.call-update
  667.1 0.0 reduce-scatter.5.cloned.1.call-start
  667.2 71.3 %reduce-scatter.3.cloned.1.call-done = f32[128,3072]{1,0:T(8,128)} async-done(((f32[512,3072]{1,0:T(8,128)}), f32[128,3072]{1,0:T(8,128)}) %reduce-scatter.3.cloned.1.call-update) | async-done | bytes 1572880 | tf_op jit(solution)/shard_map/reduce_scatter | solution.py:41
  738.5 0.0 collective-permute-done.1
  738.5 0.0 copy-done.1
  738.5 37.7 %fusion = f32[128,6144]{1,0:T(8,128)} fusion(bf16[3072,3072]{1,0:T(8,128)(2,1)} %collective-permute-done.1, bf16[3072,3072]{1,0:T(8,128)(2,1)} %maximum_select_fusion.2, pred[]{:T(512)S(6)} %eq.6, f32[128,3072]{1,0:T(8,128)} %reduce-scatter.3.cloned.1.call-done, f32[3072]{0:T(1024)S(1)} %copy-done.1), kind=kOutput, calls=%fused_computation.1 | convolution fusion | flops 5027659776 | bytes 42479616 | tf_op jit(solution)/shard_map/dot_general | solution.py:48
  776.2 0.0 reduce-scatter.5.cloned.1.call-update
  776.2 40.5 %reduce-scatter.5.cloned.1.call-done = f32[128,768]{1,0:T(8,128)} async-done(((f32[128,6144]{1,0:T(8,128)}), f32[128,768]{1,0:T(8,128)}) %reduce-scatter.5.cloned.1.call-update) | async-done | bytes 393232 | tf_op jit(solution)/shard_map/reduce_scatter | solution.py:49
  816.7 1.7 fusion.53
  (1 shorter events, 0.0 us)
Async XLA Ops:
  6.5 268.3 %all-gather.2.cloned.1.call-start = ((), (), s32[]{:S(2)}) async-start(), calls=%async_computation.3 | async-start | bytes 1769472 | tf_op jit(solution)/shard_map/all_gather | solution.py:39
  6.5 206.2 %collective-permute-start = (bf16[3072,1536]{1,0:T(8,128)(2,1)}, bf16[3072,1536]{1,0:T(8,128)(2,1)}, u32[]{:S(2)}, u32[]{:S(2)}) collective-permute-start(bf16[3072,1536]{1,0:T(8,128)(2,1)} %param.9), channel_id=1, source_target_pairs={{0,8},{8,0},{16,24},{24,16},{1,9},{9,1},{17,25},{25,17},{2,10},{10... | collective-permute-start | bytes 28311560 | tf_op jit(solution)/shard_map/ppermute | solution.py:15
  9.5 226.2 %copy-start = (bf16[128,768]{1,0:T(8,128)(2,1)S(1)}, bf16[128,768]{1,0:T(8,128)(2,1)}, u32[]{:S(2)}) copy-start(bf16[128,768]{1,0:T(8,128)(2,1)} %param.5) | copy-start | bytes 589828
  233.1 505.4 %collective-permute-start.1 = (bf16[3072,3072]{1,0:T(8,128)(2,1)}, bf16[3072,3072]{1,0:T(8,128)(2,1)}, u32[]{:S(2)}, u32[]{:S(2)}) collective-permute-start(bf16[3072,3072]{1,0:T(8,128)(2,1)} %maximum_select_fusion.2), channel_id=1, source_target_pairs={{0,16},{8,24},{16,0},{24,8},{1,17},{9,25},{17,1},{25,9},{2,18},{10... | collective-permute-start | bytes 56623112 | tf_op jit(solution)/shard_map/ppermute | solution.py:15
  252.2 486.3 %reduce-scatter.3.cloned.1.call-start = ((), (), s32[]{:S(2)}) async-start(), calls=%async_computation.4 | async-start | bytes 7864320 | tf_op jit(solution)/shard_map/reduce_scatter | solution.py:41
  667.1 71.4 %copy-start.1 = (f32[3072]{0:T(1024)S(1)}, f32[3072]{0:T(1024)}, u32[]{:S(2)}) copy-start(f32[3072]{0:T(1024)} %param.7) | copy-start | bytes 36868
  667.1 149.6 %reduce-scatter.5.cloned.1.call-start = ((), (), s32[]{:S(2)}) async-start(), calls=%async_computation.5 | async-start | bytes 3538944 | tf_op jit(solution)/shard_map/reduce_scatter | solution.py:49
Sparse Core Ops, SparseCore 0:
  252.3 22.5 all-gather.1
  667.2 71.2 reduce-scatter.2
  776.3 40.3 reduce-scatter.4
